TPU v7x, 32 devices: a whole 2x2x4 slice. The times are simulated.
32 devices in a mesh: band: 4 (over y, x), ga: 8 (over z, core).
Axes of the slice: x: 2, y: 2, z: 4, core: 2. Of those that a mesh axis runs over, the one named last changes fastest.
Arguments:
- wavefunctions: bfloat16 [512, 98304], P('band', 'ga'), may hold values from -6 to 6
- projectors: bfloat16 [2048, 98304], P('band', 'ga'), may hold values from -0.125 to 0.125
- kinetic_diag: float32 [98304], P('ga'), may hold values from 0.1 to 4
- species_index: int32 [256], replicated, may hold values from 0 to 3
- coupling: float32 [4, 8, 8], replicated, may hold values from -5 to 5
Outputs:
- applied: bfloat16 [512, 98304], P('band', 'ga')
All inputs are finite; a program needn't handle non-finite values.
Results may differ from a plain program's by a relative error of at most 0.015.
Values may be sent and summed in bfloat16 or wider, within the bound.
A program may use at most 64 MiB of HBM per device.

v0:
```python
import jax
import jax.numpy as jnp
from jax import lax
from jax.sharding import PartitionSpec as P

NPA = 8


def apply_blocks(correlations, species_index, coupling, atom_start):
    rows = correlations.shape[0]
    count = correlations.shape[1] // NPA
    local_species = lax.dynamic_slice_in_dim(species_index, atom_start, count)
    onehot = (
        local_species[:, None] == jnp.arange(coupling.shape[0], dtype=jnp.int32)[None, :]
    ).astype(jnp.float32)
    blocks = jnp.einsum("as,sij->aij", onehot, coupling, precision=lax.Precision.HIGHEST)
    mixed = jnp.einsum(
        "baj,aij->bai",
        correlations.reshape(rows, count, NPA),
        blocks,
        precision=lax.Precision.HIGHEST,
    )
    return mixed.reshape(rows, count * NPA).astype(jnp.bfloat16)


def reduce_and_mix(partial_value, species_index, coupling, first_proj):
    total = lax.psum(partial_value.astype(jnp.bfloat16), "ga").astype(jnp.float32)
    return apply_blocks(total, species_index, coupling, first_proj // NPA)


def local(wavefunctions, projectors, kinetic_diag, species_index, coupling):
    proj_local = projectors.shape[0]
    band_index = lax.axis_index("band")
    partial_value = jnp.einsum(
        "bg,pg->bp",
        lax.all_gather(wavefunctions, "band", axis=0, tiled=True),
        projectors,
        preferred_element_type=jnp.float32,
    )
    mixed = reduce_and_mix(partial_value, species_index, coupling, band_index * proj_local)
    nonlocal_term = lax.psum_scatter(
        jnp.dot(mixed, projectors, preferred_element_type=jnp.float32).astype(jnp.bfloat16),
        "band",
        scatter_dimension=0,
        tiled=True,
    ).astype(jnp.float32)
    return (kinetic_diag[None, :] * wavefunctions.astype(jnp.float32) + nonlocal_term).astype(
        jnp.bfloat16
    )


def solution(mesh):
    in_specs = (P("band", "ga"), P("band", "ga"), P("ga"), P(), P())
    out_specs = P("band", "ga")
    return jax.shard_map(local, mesh=mesh, in_specs=in_specs, out_specs=out_specs, check_vma=False)
```

profile of v0, /device:TPU:0, one launch (start us, length us, event | category | flops | bytes accessed | tf_op | source)
XLA Modules:
  0.0 351.6 jit_solution(8717082280470450847)
XLA Ops:
  6.5 0.0 copy-start
  6.5 0.0 all-gather.2.cloned.1.call-start
  6.5 0.7 all-gather.2.cloned.1.call-update
  7.3 0.0 copy-start.3
  7.3 0.0 all-reduce.2.cloned.1.call-start
  7.3 127.0 %all-gather.2.cloned.1.call-done = bf16[512,12288]{1,0:T(8,128)(2,1)} async-done(((bf16[128,12288]{1,0:T(8,128)(2,1)}), bf16[512,12288]{1,0:T(8,128)(2,1)}) %all-gather.2.cloned.1.call-update) | async-done | bytes 12582928 | tf_op jit(solution)/shard_map/all_gather | solution.py:36
  134.3 14.0 %fusion.1 = bf16[512,64,8]{0,2,1:T(8,128)(2,1)} fusion(bf16[512,12288]{1,0:T(8,128)(2,1)} %all-gather.2.cloned.1.call-done, bf16[512,12288]{1,0:T(8,128)(2,1)} %param.6), kind=kOutput, calls=%fused_computation.5 | convolution fusion | flops 6442713088 | bytes 25690112 | tf_op jit(solution)/shard_map/bg,pg->bp/dot_general | solution.py:34
  148.3 0.0 all-reduce.2.cloned.1.call-update
  148.3 0.0 reduce-scatter.2.cloned.1.call-start
  148.4 0.0 copy-done.3
  148.4 0.1 dynamic_slice.3
  148.5 0.0 copy-done
  148.5 0.2 fusion.3
  148.8 0.1 copy.7
  148.9 56.1 %all-reduce.2.cloned.1.call-done = bf16[512,64,8]{0,2,1:T(8,128)(2,1)} async-done(((bf16[512,64,8]{0,2,1:T(8,128)(2,1)}), bf16[512,64,8]{0,2,1:T(8,128)(2,1)}) %all-reduce.2.cloned.1.call-update) | async-done | bytes 524304 | tf_op jit(solution)/shard_map/psum | solution.py:27
  205.0 1.6 fusion
  206.6 14.2 %convolution_convert_fusion = bf16[512,12288]{1,0:T(8,128)(2,1)} fusion(bf16[512,512]{0,1:T(8,128)(2,1)S(1)} %fusion, bf16[512,12288]{1,0:T(8,128)(2,1)} %param.6), kind=kOutput, calls=%fused_computation | convolution fusion | flops 6448742400 | bytes 25690112 | tf_op jit(solution)/shard_map/dot_general | solution.py:42
  220.8 0.0 copy-start.1
  220.8 0.0 copy-start.2
  220.8 0.0 reduce-scatter.2.cloned.1.call-update
  220.8 119.8 %reduce-scatter.2.cloned.1.call-done = bf16[128,12288]{1,0:T(8,128)(2,1)} async-done(((bf16[512,12288]{1,0:T(8,128)(2,1)}), bf16[128,12288]{1,0:T(8,128)(2,1)}) %reduce-scatter.2.cloned.1.call-update) | async-done | bytes 3145744 | tf_op jit(solution)/shard_map/reduce_scatter | solution.py:41
  340.6 0.0 copy-done.1
  340.6 0.0 copy-done.2
  340.6 4.5 %add_convert_fusion = bf16[128,12288]{1,0:T(8,128)(2,1)} fusion(bf16[128,12288]{1,0:T(8,128)(2,1)} %reduce-scatter.2.cloned.1.call-done, bf16[128,12288]{1,0:T(8,128)(2,1)S(1)} %copy-done.1, f32[12288]{0:T(1024)S(1)} %copy-done.2), kind=kLoop, calls=%fused_computation.1 | loop fusion | flops 7864320 | bytes 9486336 | tf_op jit(solution)/shard_map/convert_element_type | solution.py:47
Async XLA Ops:
  6.5 142.0 %copy-start = (f32[4,8,8]{2,1,0:T(8,128)S(1)}, f32[4,8,8]{2,1,0:T(8,128)}, u32[]{:S(2)}) copy-start(f32[4,8,8]{2,1,0:T(8,128)} %param.9) | copy-start | bytes 3076
  6.5 127.8 %all-gather.2.cloned.1.call-start = ((), (), s32[]{:S(2)}) async-start(), calls=%async_computation.1 | async-start | bytes 15728640 | tf_op jit(solution)/shard_map/all_gather | solution.py:36
  7.3 141.2 %copy-start.3 = (s32[256]{0:T(256)S(1)}, s32[256]{0:T(256)}, u32[]{:S(2)}) copy-start(s32[256]{0:T(256)} %param.8) | copy-start | bytes 3076
  7.3 197.7 %all-reduce.2.cloned.1.call-start = ((), (), s32[]{:S(2)}) async-start(), calls=%async_computation.2 | async-start | bytes 1048576 | tf_op jit(solution)/shard_map/psum | solution.py:27
  148.3 192.3 %reduce-scatter.2.cloned.1.call-start = ((), (), s32[]{:S(2)}) async-start(), calls=%async_computation.3 | async-start | bytes 15728640 | tf_op jit(solution)/shard_map/reduce_scatter | solution.py:41
  220.8 119.9 %copy-start.1 = (bf16[128,12288]{1,0:T(8,128)(2,1)S(1)}, bf16[128,12288]{1,0:T(8,128)(2,1)}, u32[]{:S(2)}) copy-start(bf16[128,12288]{1,0:T(8,128)(2,1)} %param.5) | copy-start | bytes 9437188
  220.8 119.9 %copy-start.2 = (f32[12288]{0:T(1024)S(1)}, f32[12288]{0:T(1024)}, u32[]{:S(2)}) copy-start(f32[12288]{0:T(1024)} %param.7) | copy-start | bytes 147460
Sparse Core Ops, SparseCore 0:
  9.2 125.0 all-gather.1
  148.5 56.4 all-reduce.1
  220.9 119.6 reduce-scatter.1
where the time goes:
time: 352 us
  waiting for transfers between devices  304 us (86%)
  matrix products  30 us (9%)
  between operations  13.2 us (4%)
  other arithmetic  4.48 us (1%)
    all_gather x1, waiting for transfers between devices, local(): lax.all_gather(wavefunctions, 'band', axis=0, tiled=True)  127 us
    reduce_scatter x1, waiting for transfers between devices, local(): lax.psum_scatter(jnp.dot(mixed, projectors, preferred_element_type=jnp.fl...  120 us
    psum x1, waiting for transfers between devices, reduce_and_mix(): lax.psum(partial_value.astype(jnp.bfloat16), 'ga').astype(jnp.float32)  56.1 us
    dot_general x1, matrix products, local(): jnp.dot(mixed, projectors, preferred_element_type=jnp.float32)  14.2 us
    dot_general x1, matrix products, local(): jnp.einsum('bg,pg->bp', lax.all_gather(wavefunctions, 'band', axis=0, til...  14 us
  transfers between devices with their start and end apart: 3, of which 3 were waited for; matrix products, arithmetic and copies ran while one was open for 0% of the time, Pallas kernels for 0%

commit v1 on v0

--- a/solution.py
+++ b/solution.py
@@ -1,7 +1,15 @@
+import functools
+
 import jax
 import jax.numpy as jnp
 from jax import lax
+from jax.experimental import pallas as pl
+from jax.experimental.pallas import tpu as pltpu
 from jax.sharding import PartitionSpec as P
+
+CHUNKS = 2
+TILES = 4
+LANES = 128
 
 NPA = 8
 
@@ -49,7 +57,295 @@
     )
 
 
+def mixing_tiles(species_index, coupling, first_atom, count):
+    npa = coupling.shape[1]
+    local_species = lax.dynamic_slice_in_dim(species_index, first_atom, count)
+    onehot = (
+        local_species[:, None] == jnp.arange(coupling.shape[0], dtype=jnp.int32)[None, :]
+    ).astype(jnp.float32)
+    per_tile = LANES // npa
+    spread = jnp.einsum("as,sij->jai", onehot, coupling, precision=lax.Precision.HIGHEST)
+    spread = spread.reshape(npa, count // per_tile, LANES).transpose(1, 0, 2)
+    spread = jnp.tile(spread, (1, per_tile, 1))
+    atom_of = jnp.arange(LANES) // npa
+    return jnp.where(atom_of[:, None] == atom_of[None, :], spread, 0.0)
+
+
+def kernel(
+    nga, wf, pj, tiles, out,
+    proj, wave, acc, csend, crecv, sumf, sumb, parts, mine, theirs, nsend, nrecv, nkeep, nfull,
+    s_loc, s_p, s_wm, s_wo, s_wf, s_a, s_c, s_d, s_f, s_n, s_o,
+):
+    chunks, _, rows, half = wave.shape
+    width = nsend.shape[-1]
+    quarter = nga // 4
+    band, me = lax.axis_index("band"), lax.axis_index("ga")
+    core, y, x = me % 2, band // 2, band % 2
+    across_x, across_y, diag = y * 2 + 1 - x, (1 - y) * 2 + x, 3 - band
+    m = (1 - core) * y + core * x
+    m_nbr = (1 - core) * across_y + core * across_x
+    o_nbr = (1 - core) * across_x + core * across_y
+    here = pl.multiple_of(m * half, LANES)
+    there = pl.multiple_of((1 - m) * half, LANES)
+    to_m, to_o = {"band": m_nbr}, {"band": o_nbr}
+
+    def remote(src, dst, sems, device):
+        return pltpu.make_async_remote_copy(
+            src_ref=src, dst_ref=dst, send_sem=sems.at[0], recv_sem=sems.at[1],
+            device_id=device, device_id_type=pl.DeviceIdType.MESH,
+        )
+
+    def span(k):
+        return pl.ds(k * rows, rows)
+
+    local_p = pltpu.make_async_copy(pj.at[:, pl.ds(here, half)], proj.at[0], s_loc.at[0])
+    local_w = [
+        pltpu.make_async_copy(wf.at[span(k), pl.ds(here, half)], wave.at[k, band], s_loc.at[1 + k])
+        for k in range(chunks)
+    ]
+    send_p = remote(pj.at[:, pl.ds(there, half)], proj.at[1], s_p, to_m)
+    send_wm = [
+        remote(wf.at[span(k), pl.ds(there, half)], wave.at[k, band], s_wm.at[k], to_m)
+        for k in range(chunks)
+    ]
+    send_wo = [
+        remote(wf.at[span(k), pl.ds(here, half)], wave.at[k, band], s_wo.at[k], to_o)
+        for k in range(chunks)
+    ]
+    send_wf = [
+        remote(wave.at[k, m_nbr], wave.at[k, m_nbr], s_wf.at[k], to_o) for k in range(chunks)
+    ]
+    send_a = [remote(csend.at[k], crecv.at[k], s_a.at[k], to_m) for k in range(chunks)]
+    send_f = [remote(mine.at[k], theirs.at[k], s_f.at[k], to_m) for k in range(chunks)]
+
+    def peer(step):
+        return (me + step + 1) % nga
+
+    def send_c(k, step):
+        return remote(
+            sumb.at[k, peer(step)], parts.at[k, step], s_c.at[k, step], {"ga": peer(step)}
+        )
+
+    def send_d(k, step):
+        return remote(mine.at[k, me], mine.at[k, me], s_d.at[k, step], {"ga": peer(step)})
+
+    def send_n(k, t):
+        return remote(nsend.at[k, t], nrecv.at[k, t], s_n.at[k, t], to_o)
+
+    def send_o(k, t):
+        place = out.at[span(k), pl.ds(pl.multiple_of(here + t * width, LANES), width)]
+        return remote(nfull.at[k, t], place, s_o.at[k, t], to_m)
+
+    def each_peer(body):
+        def step(i, carry):
+            body(i)
+            return carry
+
+        lax.fori_loop(0, nga - 1, step, 0)
+
+    def each_tile(body, first=0, last=TILES):
+        def step(i, carry):
+            body(i)
+            return carry
+
+        lax.fori_loop(first, last, step, 0)
+
+    def correlate(k, slot):
+        acc[...] = jnp.zeros_like(acc)
+
+        def tile(t):
+            cols = pl.ds(pl.multiple_of(t * width, LANES), width)
+            acc[...] += lax.dot_general(
+                wave[k, :, :, cols].reshape(4 * rows, width),
+                proj[slot, :, cols],
+                (((1,), (1,)), ((), ())),
+                preferred_element_type=jnp.float32,
+            )
+
+        each_tile(tile)
+
+    def first(k):
+        local_w[k].wait()
+        send_wo[k].wait_recv()
+        send_wf[k].wait_recv()
+        correlate(k, 1)
+        csend[k] = acc[...].astype(jnp.bfloat16)
+        send_a[k].start()
+        correlate(k, 0)
+        sumf[k] = acc[...].reshape(sumf.shape[1:])
+
+    def reduce_start(k):
+        send_a[k].wait_recv()
+        total = sumf[k] + crecv[k].astype(jnp.float32).reshape(sumf.shape[1:])
+        sumf[k] = total
+        sumb[k] = total.astype(jnp.bfloat16)
+        each_peer(lambda step: send_c(k, step).start())
+
+    def mix_start(k):
+        each_peer(lambda step: send_c(k, step).wait_recv())
+        total = sumf[k, me]
+        for step in range(nga - 1):
+            total = total + parts[k, step].astype(jnp.float32)
+        for t in range(tiles.shape[0]):
+            cols = slice(t * LANES, (t + 1) * LANES)
+            mine[k, me, :, cols] = jnp.dot(
+                total[:, cols], tiles[t],
+                preferred_element_type=jnp.float32, precision=lax.Precision.HIGHEST,
+            ).astype(jnp.bfloat16)
+        each_peer(lambda step: send_d(k, step).start())
+
+    def share_start(k):
+        each_peer(lambda step: send_d(k, step).wait_recv())
+        send_f[k].start()
+
+    def second(k):
+        send_f[k].wait_recv()
+
+        def ordered(ref):
+            picks = [ref[k, pl.ds(b * quarter, quarter)] for b in (o_nbr, diag, band, m_nbr)]
+            return jnp.concatenate(picks, axis=0).reshape(4 * rows, ref.shape[-1])
+
+        def tile(t):
+            cols = pl.ds(pl.multiple_of(t * width, LANES), width)
+            value = jnp.dot(ordered(mine), proj[0, :, cols], preferred_element_type=jnp.float32)
+            value += jnp.dot(ordered(theirs), proj[1, :, cols], preferred_element_type=jnp.float32)
+            value = value.reshape(4, rows, width)
+            nsend[k, t] = value[:2].astype(jnp.bfloat16)
+            send_n(k, t).start()
+            nkeep[k, t] = value[2:]
+
+        each_tile(tile)
+
+    def finish(k, begin, end):
+        def tile(t):
+            send_n(k, t).wait_recv()
+            nfull[k, t] = (nkeep[k, t, 1] + nrecv[k, t, 1].astype(jnp.float32)).astype(jnp.bfloat16)
+            send_o(k, t).start()
+            cols = pl.ds(pl.multiple_of(here + t * width, LANES), width)
+            out[span(k), cols] = (nkeep[k, t, 0] + nrecv[k, t, 0].astype(jnp.float32)).astype(
+                jnp.bfloat16
+            )
+
+        each_tile(tile, begin, end)
+
+    local_p.start()
+    for k in range(chunks):
+        local_w[k].start()
+    barrier = pltpu.get_barrier_semaphore()
+    for device in (to_m, to_o):
+        pl.semaphore_signal(
+            barrier, inc=1, device_id=device, device_id_type=pl.DeviceIdType.MESH
+        )
+    each_peer(
+        lambda step: pl.semaphore_signal(
+            barrier, inc=1, device_id={"ga": peer(step)}, device_id_type=pl.DeviceIdType.MESH
+        )
+    )
+    pl.semaphore_wait(barrier, nga + 1)
+
+    send_wm[0].start()
+    send_wo[0].start()
+    send_p.start()
+    for k in range(1, chunks):
+        send_wm[k].start()
+    send_wm[0].wait_recv()
+    send_wf[0].start()
+    local_p.wait()
+    send_p.wait_recv()
+    for k in range(1, chunks):
+        send_wo[k].start()
+
+    first(0)
+    reduce_start(0)
+    for k in range(1, chunks):
+        send_wm[k].wait_recv()
+        send_wf[k].start()
+    mix_start(0)
+    for k in range(1, chunks):
+        first(k)
+        share_start(k - 1)
+        reduce_start(k)
+        second(k - 1)
+        mix_start(k)
+        finish(k - 1, 0, TILES // 2)
+        if k == chunks - 1:
+            share_start(k)
+        finish(k - 1, TILES // 2, TILES)
+    if chunks == 1:
+        share_start(0)
+    second(chunks - 1)
+    finish(chunks - 1, 0, TILES)
+
+    send_p.wait_send()
+    for k in range(chunks):
+        for copy in (send_wm[k], send_wo[k], send_wf[k], send_a[k], send_f[k]):
+            copy.wait_send()
+        each_peer(lambda step: send_c(k, step).wait_send())
+        each_peer(lambda step: send_d(k, step).wait_send())
+        each_tile(lambda t: send_n(k, t).wait_send())
+        each_tile(lambda t: send_o(k, t).wait())
+
+
+def square(nga, wavefunctions, projectors, kinetic_diag, species_index, coupling):
+    bands, waves = wavefunctions.shape
+    count = projectors.shape[0]
+    npa = coupling.shape[1]
+    half, rows = waves // 2, bands // CHUNKS
+    width, share = half // TILES, 4 * rows // nga
+    tiles = mixing_tiles(
+        species_index, coupling, lax.axis_index("band") * (count // npa), count // npa
+    )
+    bf16, f32 = jnp.bfloat16, jnp.float32
+    dma = pltpu.SemaphoreType.DMA
+    nonlocal_term = pl.pallas_call(
+        functools.partial(kernel, nga),
+        out_shape=jax.ShapeDtypeStruct((bands, waves), bf16),
+        in_specs=[
+            pl.BlockSpec(memory_space=pl.ANY),
+            pl.BlockSpec(memory_space=pl.ANY),
+            pl.BlockSpec(memory_space=pltpu.VMEM),
+        ],
+        out_specs=pl.BlockSpec(memory_space=pltpu.VMEM),
+        scratch_shapes=[
+            pltpu.VMEM((2, count, half), bf16),
+            pltpu.VMEM((CHUNKS, 4, rows, half), bf16),
+            pltpu.VMEM((4 * rows, count), f32),
+            pltpu.VMEM((CHUNKS, 4 * rows, count), bf16),
+            pltpu.VMEM((CHUNKS, 4 * rows, count), bf16),
+            pltpu.VMEM((CHUNKS, nga, share, count), f32),
+            pltpu.VMEM((CHUNKS, nga, share, count), bf16),
+            pltpu.VMEM((CHUNKS, nga - 1, share, count), bf16),
+            pltpu.VMEM((CHUNKS, nga, share, count), bf16),
+            pltpu.VMEM((CHUNKS, nga, share, count), bf16),
+            pltpu.VMEM((CHUNKS, TILES, 2, rows, width), bf16),
+            pltpu.VMEM((CHUNKS, TILES, 2, rows, width), bf16),
+            pltpu.VMEM((CHUNKS, TILES, 2, rows, width), f32),
+            pltpu.VMEM((CHUNKS, TILES, rows, width), bf16),
+            dma((1 + CHUNKS,)),
+            dma((2,)),
+            dma((CHUNKS, 2)),
+            dma((CHUNKS, 2)),
+            dma((CHUNKS, 2)),
+            dma((CHUNKS, 2)),
+            dma((CHUNKS, nga - 1, 2)),
+            dma((CHUNKS, nga - 1, 2)),
+            dma((CHUNKS, 2)),
+            dma((CHUNKS, TILES, 2)),
+            dma((CHUNKS, TILES, 2)),
+        ],
+        compiler_params=pltpu.CompilerParams(
+            collective_id=0, has_side_effects=True, vmem_limit_bytes=60 * 2**20
+        ),
+    )(wavefunctions, projectors, tiles)
+    return (
+        kinetic_diag[None, :] * wavefunctions.astype(f32) + nonlocal_term.astype(f32)
+    ).astype(bf16)
+
+
 def solution(mesh):
     in_specs = (P("band", "ga"), P("band", "ga"), P("ga"), P(), P())
     out_specs = P("band", "ga")
-    return jax.shard_map(local, mesh=mesh, in_specs=in_specs, out_specs=out_specs, check_vma=False)
+    nga = mesh.shape["ga"]
+    fits = mesh.shape["band"] == 4 and nga % 4 == 0
+    body = functools.partial(square, nga) if fits else local
+    return jax.shard_map(body, mesh=mesh, in_specs=in_specs, out_specs=out_specs, check_vma=False)

time: 352 us -> 217 us (0.62)
  waiting for transfers between devices: 304 us -> 0 us
  Pallas kernels: 0 us -> 210 us
  matrix products: 30 us -> 0.21 us
  between operations: 13.2 us -> 0.07 us
    pallas_call x0 -> x1, Pallas kernels: none -> 210 us  [square(): pl.pallas_call(functools.partial(kernel, nga), out_shape=jax.ShapeDtypeSt...]
    all_gather x1 -> x0, waiting for transfers between devices: 127 us -> none  [local(): lax.all_gather(wavefunctions, 'band', axis=0, tiled=True)]
    reduce_scatter x1 -> x0, waiting for transfers between devices: 120 us -> none  [local(): lax.psum_scatter(jnp.dot(mixed, projectors, preferred_element_type=jnp.fl...]
    psum x1 -> x0, waiting for transfers between devices: 56.1 us -> none  [reduce_and_mix(): lax.psum(partial_value.astype(jnp.bfloat16), 'ga').astype(jnp.float32)]
    dot_general x4 -> x1, matrix products: 30 us -> 0.21 us  [mixing_tiles(): jnp.einsum('as,sij->jai', onehot, coupling, precision=lax.Precision.HIGHEST)]
  transfers between devices with their start and end apart: 3 -> 0, of which waited for: 3 -> 0; matrix products, arithmetic and copies ran while one was open for 0% -> 0% of each run, Pallas kernels for 0% -> 0%
where the time goes in v1:
time: 217 us; the launch traced here: 216 us
  Pallas kernels  210 us (97%)
  other arithmetic  5.29 us (2%)
    pallas_call x1, Pallas kernels, square(): pl.pallas_call(functools.partial(kernel, nga), out_shape=jax.ShapeDtypeSt...  210 us
    convert_element_type x1, other arithmetic, square(): return (kinetic_diag[None, :] * wavefunctions.astype(f32) + nonlocal_term...  4.48 us

profile of v1, /device:TPU:0, one launch (start us, length us, event | category | flops | bytes accessed | tf_op | source)
XLA Modules:
  0.0 216.4 jit_solution(7492640827841169023)
XLA Ops:
  0.0 0.0 copy-start
  0.0 0.8 dynamic_slice.3
  0.8 0.1 broadcast_compare_fusion
  0.9 0.0 copy-done
  0.9 0.2 convolution_bitcast_fusion
  1.1 0.1 copy.8
  1.2 0.2 reshape.35
  1.4 0.7 bitcast_select_fusion.tiles
  2.1 0.0 copy-start.1
  2.1 0.0 copy-start.2
  2.1 209.7 %shard_map.55 = bf16[128,12288]{1,0:T(8,128)(2,1)} custom-call(bf16[128,12288]{1,0:T(8,128)(2,1)} %wf.1, bf16[512,12288]{1,0:T(8,128)(2,1)} %pj.1, f32[4,128,128]{2,1,0:T(8,128)} %bitcast_select_fusion.tiles), custom_call_target="tpu_custom_call" | custom-call | tf_op jit(solution)/shard_map/pallas_call | solution.py:300
  211.9 0.0 copy-done.1
  211.9 0.0 copy-done.2
  211.9 4.5 %add_convert_fusion = bf16[128,12288]{1,0:T(8,128)(2,1)} fusion(bf16[128,12288]{1,0:T(8,128)(2,1)} %shard_map.55, bf16[128,12288]{1,0:T(8,128)(2,1)S(1)} %copy-done.1, f32[12288]{0:T(1024)S(1)} %copy-done.2), kind=kLoop, calls=%fused_computation | loop fusion | flops 7864320 | bytes 9486336 | tf_op jit(solution)/shard_map/convert_element_type | solution.py:342
  (2 shorter events, 0.0 us)
Async XLA Ops:
  0.0 0.9 copy-start
  2.1 209.8 %copy-start.1 = (bf16[128,12288]{1,0:T(8,128)(2,1)S(1)}, bf16[128,12288]{1,0:T(8,128)(2,1)}, u32[]{:S(2)}) copy-start(bf16[128,12288]{1,0:T(8,128)(2,1)} %wf.1) | copy-start | bytes 9437188
  2.1 209.8 %copy-start.2 = (f32[12288]{0:T(1024)S(1)}, f32[12288]{0:T(1024)}, u32[]{:S(2)}) copy-start(f32[12288]{0:T(1024)} %param.7) | copy-start | bytes 147460

commit v2 on v1

--- a/solution.py
+++ b/solution.py
@@ -73,7 +73,7 @@
 
 def kernel(
     nga, wf, pj, tiles, out,
-    proj, wave, acc, csend, crecv, sumf, sumb, parts, mine, theirs, nsend, nrecv, nkeep, nfull,
+    proj, wave, acc, csend, crecv, sumf, sumb, parts, mine, theirs, nsend, nrecv, nfull,
     s_loc, s_p, s_wm, s_wo, s_wf, s_a, s_c, s_d, s_f, s_n, s_o,
 ):
     chunks, _, rows, half = wave.shape
@@ -168,11 +168,16 @@
         local_w[k].wait()
         send_wo[k].wait_recv()
         send_wf[k].wait_recv()
+        if k == 0:
+            correlate(k, 0)
+            sumf[k] = acc[...].reshape(sumf.shape[1:])
+            send_p.wait_recv()
         correlate(k, 1)
         csend[k] = acc[...].astype(jnp.bfloat16)
         send_a[k].start()
-        correlate(k, 0)
-        sumf[k] = acc[...].reshape(sumf.shape[1:])
+        if k > 0:
+            correlate(k, 0)
+            sumf[k] = acc[...].reshape(sumf.shape[1:])
 
     def reduce_start(k):
         send_a[k].wait_recv()
@@ -198,33 +203,38 @@
         each_peer(lambda step: send_d(k, step).wait_recv())
         send_f[k].start()
 
+    def ordered(ref, k, blocks):
+        picks = [ref[k, pl.ds(b * quarter, quarter)] for b in blocks]
+        return jnp.concatenate(picks, axis=0).reshape(2 * rows, ref.shape[-1])
+
+    def expand(k, t, blocks):
+        cols = pl.ds(pl.multiple_of(t * width, LANES), width)
+        value = jnp.dot(
+            ordered(mine, k, blocks), proj[0, :, cols], preferred_element_type=jnp.float32
+        )
+        value += jnp.dot(
+            ordered(theirs, k, blocks), proj[1, :, cols], preferred_element_type=jnp.float32
+        )
+        return value.reshape(2, rows, width)
+
     def second(k):
         send_f[k].wait_recv()
 
-        def ordered(ref):
-            picks = [ref[k, pl.ds(b * quarter, quarter)] for b in (o_nbr, diag, band, m_nbr)]
-            return jnp.concatenate(picks, axis=0).reshape(4 * rows, ref.shape[-1])
-
         def tile(t):
-            cols = pl.ds(pl.multiple_of(t * width, LANES), width)
-            value = jnp.dot(ordered(mine), proj[0, :, cols], preferred_element_type=jnp.float32)
-            value += jnp.dot(ordered(theirs), proj[1, :, cols], preferred_element_type=jnp.float32)
-            value = value.reshape(4, rows, width)
-            nsend[k, t] = value[:2].astype(jnp.bfloat16)
+            nsend[k, t] = expand(k, t, (o_nbr, diag)).astype(jnp.bfloat16)
             send_n(k, t).start()
-            nkeep[k, t] = value[2:]
 
         each_tile(tile)
 
     def finish(k, begin, end):
         def tile(t):
+            value = expand(k, t, (band, m_nbr))
             send_n(k, t).wait_recv()
-            nfull[k, t] = (nkeep[k, t, 1] + nrecv[k, t, 1].astype(jnp.float32)).astype(jnp.bfloat16)
+            value += nrecv[k, t].astype(jnp.float32)
+            nfull[k, t] = value[1].astype(jnp.bfloat16)
             send_o(k, t).start()
             cols = pl.ds(pl.multiple_of(here + t * width, LANES), width)
-            out[span(k), cols] = (nkeep[k, t, 0] + nrecv[k, t, 0].astype(jnp.float32)).astype(
-                jnp.bfloat16
-            )
+            out[span(k), cols] = value[0].astype(jnp.bfloat16)
 
         each_tile(tile, begin, end)
 
@@ -250,10 +260,9 @@
         send_wm[k].start()
     send_wm[0].wait_recv()
     send_wf[0].start()
-    local_p.wait()
-    send_p.wait_recv()
     for k in range(1, chunks):
         send_wo[k].start()
+    local_p.wait()
 
     first(0)
     reduce_start(0)
@@ -262,10 +271,10 @@
         send_wf[k].start()
     mix_start(0)
     for k in range(1, chunks):
+        share_start(k - 1)
         first(k)
-        share_start(k - 1)
+        second(k - 1)
         reduce_start(k)
-        second(k - 1)
         mix_start(k)
         finish(k - 1, 0, TILES // 2)
         if k == chunks - 1:
@@ -319,7 +328,6 @@
             pltpu.VMEM((CHUNKS, nga, share, count), bf16),
             pltpu.VMEM((CHUNKS, TILES, 2, rows, width), bf16),
             pltpu.VMEM((CHUNKS, TILES, 2, rows, width), bf16),
-            pltpu.VMEM((CHUNKS, TILES, 2, rows, width), f32),
             pltpu.VMEM((CHUNKS, TILES, rows, width), bf16),
             dma((1 + CHUNKS,)),
             dma((2,)),

time: 217 us -> 207 us (0.954)
  Pallas kernels: 210 us -> 200 us
    pallas_call x1, Pallas kernels: 210 us -> 200 us  [square(): pl.pallas_call(functools.partial(kernel, nga), out_shape=jax.ShapeDtypeSt...]
where the time goes in v2:
time: 207 us
  Pallas kernels  200 us (97%)
  other arithmetic  5.29 us (3%)
    pallas_call x1, Pallas kernels, square(): pl.pallas_call(functools.partial(kernel, nga), out_shape=jax.ShapeDtypeSt...  200 us
    convert_element_type x1, other arithmetic, square(): return (kinetic_diag[None, :] * wavefunctions.astype(f32) + nonlocal_term...  4.48 us

profile of v2, /device:TPU:0, one launch (start us, length us, event | category | flops | bytes accessed | tf_op | source)
XLA Modules:
  0.0 206.6 jit_solution(18082992797426148529)
XLA Ops:
  0.0 0.0 copy-start
  0.0 0.8 dynamic_slice.3
  0.8 0.1 broadcast_compare_fusion
  0.9 0.0 copy-done
  0.9 0.2 convolution_bitcast_fusion
  1.1 0.1 copy.8
  1.2 0.2 reshape.35
  1.4 0.7 bitcast_select_fusion.tiles
  2.1 0.0 copy-start.1
  2.1 0.0 copy-start.2
  2.1 199.9 %shard_map.55 = bf16[128,12288]{1,0:T(8,128)(2,1)} custom-call(bf16[128,12288]{1,0:T(8,128)(2,1)} %wf.1, bf16[512,12288]{1,0:T(8,128)(2,1)} %pj.1, f32[4,128,128]{2,1,0:T(8,128)} %bitcast_select_fusion.tiles), custom_call_target="tpu_custom_call" | custom-call | tf_op jit(solution)/shard_map/pallas_call | solution.py:309
  202.1 0.0 copy-done.1
  202.1 0.0 copy-done.2
  202.1 4.5 %add_convert_fusion = bf16[128,12288]{1,0:T(8,128)(2,1)} fusion(bf16[128,12288]{1,0:T(8,128)(2,1)} %shard_map.55, bf16[128,12288]{1,0:T(8,128)(2,1)S(1)} %copy-done.1, f32[12288]{0:T(1024)S(1)} %copy-done.2), kind=kLoop, calls=%fused_computation | loop fusion | flops 7864320 | bytes 9486336 | tf_op jit(solution)/shard_map/convert_element_type | solution.py:350
  (2 shorter events, 0.0 us)
Async XLA Ops:
  0.0 0.9 copy-start
  2.1 200.0 %copy-start.1 = (bf16[128,12288]{1,0:T(8,128)(2,1)S(1)}, bf16[128,12288]{1,0:T(8,128)(2,1)}, u32[]{:S(2)}) copy-start(bf16[128,12288]{1,0:T(8,128)(2,1)} %wf.1) | copy-start | bytes 9437188
  2.1 200.0 %copy-start.2 = (f32[12288]{0:T(1024)S(1)}, f32[12288]{0:T(1024)}, u32[]{:S(2)}) copy-start(f32[12288]{0:T(1024)} %param.7) | copy-start | bytes 147460
